TPU v7x, 32 devices: a whole 2x2x4 slice. The times are simulated.
32 devices in a mesh: dp: 8 (over z, core), mp: 4 (over y, x).
Axes of the slice: x: 2, y: 2, z: 4, core: 2. Of those that a mesh axis runs over, the one named last changes fastest.
Arguments:
- patches: bfloat16 [256, 256, 1280], P(('dp', 'mp')), may hold values from -6 to 6
- position: bfloat16 [256, 1280], replicated, may hold values from -3 to 3
- keep: int32 [256, 64], P(('dp', 'mp')), may hold values from 0 to 255, as said below
- counts: int32 [256], replicated, may hold values from 1 to 64, as said below
- offsets: int32 [256], replicated, may hold values from 0 to 10239, as said below
- ln_gain: float32 [1, 2, 1280], replicated, may hold values from 0.25 to 1.75
- ln_bias: float32 [1, 2, 1280], replicated, may hold values from -2 to 2
- w_qkv: bfloat16 [1, 3, 1280, 1280], P(None, None, 'dp', 'mp')
- b_qkv: float32 [1, 3, 1280], P(None, None, 'mp'), may hold values from -3 to 3
- w_o: bfloat16 [1, 1280, 1280], P(None, 'mp', 'dp'), may hold values from -0.15625 to 0.15625
- b_o: float32 [1, 1280], replicated, may hold values from -1.5 to 1.5
- w_up: bfloat16 [1, 1280, 5120], P(None, 'dp', 'mp'), may hold values from -0.15625 to 0.15625
- b_up: float32 [1, 5120], P(None, 'mp'), may hold values from -3 to 3
- w_down: bfloat16 [1, 5120, 1280], P(None, 'mp', 'dp'), may hold values from -0.078125 to 0.078125
- b_down: float32 [1, 1280], replicated, may hold values from -1.5 to 1.5
Outputs:
- encoded: bfloat16 [10240, 1280], P(('dp', 'mp'))
Inputs may be any that keep to these rules, and one draw needn't show every extreme that they name: `keep`: the first counts[i] entries of row i are distinct and name image i's visible patches; later entries are unused. `counts`: some image has exactly 64 visible patches. Image i, held by dp index s = i // 32, occupies packed rows offsets[i] to offsets[i] + counts[i] - 1, all inside the aligned block of 160 rows numbered d * 8 + s for some shard d; no two images share a row.
All inputs are finite; a program needn't handle non-finite values.
Results may differ from a plain program's by a relative error of at most 0.015.
Values may be sent and summed in bfloat16 or wider, within the bound.
A program may use at most 64 MiB of HBM per device.

v0:
```python
import math
import jax
import jax.numpy as jnp
from jax import lax
from jax.sharding import PartitionSpec as P

HEAD = 80


def norm_rows(values, gain_row, shift_row):
    row_mean = jnp.mean(values, axis=-1, keepdims=True)
    centred = values - row_mean
    spread = jnp.mean(centred * centred, axis=-1, keepdims=True)
    return (centred * lax.rsqrt(spread + 1e-06) * gain_row + shift_row).astype(jnp.bfloat16)


def gather_rows(normed):
    return lax.all_gather(normed, "mp", axis=0, tiled=True)


def fold_rows(gathered, weight):
    return jnp.einsum(
        "rd,tdc->trc",
        gathered,
        lax.all_gather(weight, "dp", axis=1, tiled=True),
        preferred_element_type=jnp.float32,
    )


def project_sum(left, weight):
    partials = jnp.dot(
        left, lax.all_gather(weight, "dp", axis=1, tiled=True), preferred_element_type=jnp.float32
    )
    return lax.psum_scatter(
        partials.astype(jnp.bfloat16), "mp", scatter_dimension=0, tiled=True
    ).astype(jnp.float32)


def attend(projected, labels, block_rows):
    row_count = projected.shape[1]
    blocks = row_count // block_rows
    head_count = projected.shape[2] // HEAD
    shaped = projected.reshape(3, blocks, block_rows, head_count, HEAD)
    scores = jnp.einsum(
        "bqhe,bkhe->bhqk", shaped[0], shaped[1], preferred_element_type=jnp.float32
    ) * (1.0 / math.sqrt(HEAD))
    labels_block = labels.reshape(blocks, block_rows)
    matches = labels_block[:, None, :, None] == labels_block[:, None, None, :]
    scores = jnp.where(matches, scores, -jnp.inf)
    row_max = jnp.max(scores, axis=-1, keepdims=True)
    weights = jnp.exp(scores - row_max)
    probabilities = (weights / jnp.sum(weights, axis=-1, keepdims=True)).astype(jnp.bfloat16)
    attended = jnp.einsum(
        "bhqk,bkhe->bqhe", probabilities, shaped[2], preferred_element_type=jnp.float32
    )
    return attended.reshape(row_count, head_count * HEAD).astype(jnp.bfloat16)


def group_rows(item_count, unit_rows):
    factor = 1
    while item_count % (factor * 2) == 0 and factor * unit_rows < 512:
        factor = factor * 2
    return factor * unit_rows


def run_layers(
    stream, labels, block_rows, ln_gain, ln_bias, w_qkv, b_qkv, w_o, b_o, w_up, b_up, w_down, b_down
):
    normed = norm_rows(stream.astype(jnp.float32), ln_gain[0, 0], ln_bias[0, 0])
    projected = (fold_rows(gather_rows(normed), w_qkv[0]) + b_qkv[0][:, None, :]).astype(
        jnp.bfloat16
    )
    attended = attend(projected, labels, block_rows)
    residual = stream.astype(jnp.float32) + project_sum(attended, w_o[0]) + b_o[0]
    normed_mlp = norm_rows(residual, ln_gain[0, 1], ln_bias[0, 1])
    up_proj = fold_rows(gather_rows(normed_mlp), w_up[0][None])[0] + b_up[0]
    hidden = jax.nn.gelu(up_proj, approximate=False).astype(jnp.bfloat16)
    stream = (residual + project_sum(hidden, w_down[0]) + b_down[0]).astype(jnp.bfloat16)
    return stream


def per_device(
    patches,
    position,
    keep,
    counts,
    offsets,
    ln_gain,
    ln_bias,
    w_qkv,
    b_qkv,
    w_o,
    b_o,
    w_up,
    b_up,
    w_down,
    b_down,
):
    local_images = patches.shape[0]
    keep_most = keep.shape[1]
    column_count = patches.shape[2]
    shard_count = lax.axis_size("dp")
    group_size = lax.axis_size("mp")
    images_here = local_images * group_size
    per_slot = (images_here + shard_count - 1) // shard_count
    slot_rows = max(keep_most + 16, per_slot * keep_most * 5 // 8)
    pack_rows = slot_rows * shard_count
    local_rows = pack_rows // group_size
    dp_index = lax.axis_index("dp")
    mp_index = lax.axis_index("mp")
    first_image = dp_index * images_here
    group_counts = lax.dynamic_slice_in_dim(counts, first_image, images_here)
    group_offsets = lax.dynamic_slice_in_dim(offsets, first_image, images_here)
    picked = jnp.take_along_axis(patches, keep[:, :, None], axis=1)
    placed = jnp.take(position, keep, axis=0)
    tokens = (picked.astype(jnp.float32) + placed.astype(jnp.float32)).astype(jnp.bfloat16)
    positions_in = jnp.arange(keep_most, dtype=jnp.int32)
    group_live = positions_in[None, :] < group_counts[:, None]
    shard_index = group_offsets // pack_rows
    base_row = (
        shard_index * slot_rows + group_offsets - shard_index * pack_rows - dp_index * slot_rows
    )
    target = jnp.where(group_live, base_row[:, None] + positions_in[None, :], pack_rows).reshape(-1)
    layer_weights = (ln_gain, ln_bias, w_qkv, b_qkv, w_o, b_o, w_up, b_up, w_down, b_down)
    image_ids = jnp.arange(counts.shape[0], dtype=jnp.int32)
    packed_rows = dp_index * pack_rows + jnp.arange(pack_rows, dtype=jnp.int32)
    inside = (packed_rows[:, None] >= offsets[None, :]) & (
        packed_rows[:, None] < (offsets + counts)[None, :]
    )
    labels = jnp.max(jnp.where(inside, image_ids[None, :] + 1, 0), axis=1) - 1
    featured = lax.all_to_all(
        tokens.reshape(-1, column_count), "mp", split_axis=1, concat_axis=0, tiled=True
    )
    buffer_rows = (
        jnp.zeros((pack_rows, featured.shape[1]), jnp.bfloat16)
        .at[target]
        .set(featured, mode="drop")
    )
    stream = lax.all_to_all(
        lax.all_to_all(buffer_rows, "dp", split_axis=0, concat_axis=0, tiled=True),
        "mp",
        split_axis=0,
        concat_axis=1,
        tiled=True,
    )
    stream = run_layers(stream, labels, group_rows(shard_count, slot_rows), *layer_weights)
    own_labels = lax.dynamic_slice_in_dim(labels, mp_index * local_rows, local_rows)
    output = jnp.where(own_labels[:, None] >= 0, stream, jnp.zeros_like(stream))
    return output


def solution(mesh):
    in_specs = (
        P(("dp", "mp"), None, None),
        P(),
        P(("dp", "mp"), None),
        P(),
        P(),
        P(),
        P(),
        P(None, None, "dp", "mp"),
        P(None, None, "mp"),
        P(None, "mp", "dp"),
        P(),
        P(None, "dp", "mp"),
        P(None, "mp"),
        P(None, "mp", "dp"),
        P(),
    )
    out_specs = P(("dp", "mp"), None)
    return jax.shard_map(
        per_device, mesh=mesh, in_specs=in_specs, out_specs=out_specs, check_vma=False
    )
```

profile of v0, /device:TPU:0, one launch (start us, length us, event | category | flops | bytes accessed | tf_op | source)
XLA Modules:
  0.0 429.3 jit_solution(11046292865014236250)
XLA Ops:
  8.8 2.1 gather_fusion
  10.9 1.5 copy.54
  12.5 8.7 %gather_fusion.1 = bf16[512,1280]{1,0:T(8,128)(2,1)S(1)} fusion(bf16[8,256,1280]{2,1,0:T(8,128)(2,1)} %param.15, s32[512]{0:T(512)S(1)} %reshape.190), kind=kCustom, calls=%fused_computation.1 | custom fusion | bytes 2625536 | tf_op jit(solution)/shard_map/jit(take_along_axis)/gather | solution.py:114
  21.1 1.5 copy.53
  22.7 3.3 add_convert_fusion.1
  26.0 5.2 %all-to-all-start = ((bf16[512,4,320]{0,2,1:T(8,128)(2,1)}), bf16[512,4,320]{0,2,1:T(8,128)(2,1)S(1)}, u32[]{:S(2)}, u32[]{:S(2)}) async-start(bf16[512,4,320]{0,2,1:T(8,128)(2,1)} %add_convert_fusion.1), calls=%async_computation | async-start | bytes 2621440 | tf_op jit(solution)/shard_map/all_to_all | solution.py:131
  32.2 15.4 %all-to-all-done = bf16[512,4,320]{0,2,1:T(8,128)(2,1)S(1)} async-done(((bf16[512,4,320]{0,2,1:T(8,128)(2,1)}), bf16[512,4,320]{0,2,1:T(8,128)(2,1)S(1)}, u32[]{:S(2)}, u32[]{:S(2)}) %all-to-all-start) | async-done | bytes 1310752 | tf_op jit(solution)/shard_map/all_to_all | solution.py:131
  47.6 1.6 copy.65
  49.2 10.0 %scatter_custom_fusion = bf16[1280,320]{1,0:T(8,128)(2,1)S(1)} fusion(s32[2048]{0:T(1024)S(1)} %bitcast.59, bf16[2048,320]{1,0:T(8,128)(2,1)} %bitcast.57, bf16[]{:T(256)} %constant.58.clone.1), kind=kCustom, calls=%fused_computation.64 | custom fusion | bytes 819712 | tf_op jit(solution)/shard_map/scatter | solution.py:137
  59.2 32.4 %all_to_all.38 = bf16[8,160,320]{2,1,0:T(8,128)(2,1)} all-to-all(bf16[8,160,320]{2,1,0:T(8,128)(2,1)S(1)} %bitcast.55), channel_id=1, replica_groups=mesh['dp'=8,'mp'=4] {'dp'}, dimensions={0} | all-to-all | bytes 1638400 | tf_op jit(solution)/shard_map/all_to_all | solution.py:140
  91.6 3.6 all-to-all-start.2
  95.3 13.2 %all-to-all-done.2 = bf16[4,320,320]{2,1,0:T(8,128)(2,1)S(1)} async-done(((bf16[4,320,320]{2,1,0:T(8,128)(2,1)}), bf16[4,320,320]{2,1,0:T(8,128)(2,1)S(1)}, u32[]{:S(2)}, u32[]{:S(2)}) %all-to-all-start.2) | async-done | bytes 819232 | tf_op jit(solution)/shard_map/all_to_all | solution.py:139
  108.6 2.5 copy.57
  111.2 2.4 reshape.181
  117.6 17.2 %all-gather.1 = bf16[1,320,1280]{1,2,0:T(8,128)(2,1)} all-gather(bf16[1,320,160]{1,2,0:T(8,128)(2,1)S(1)} %copy-done.5), channel_id=3, replica_groups=mesh['dp'=8,'mp'=4] {'dp'}, dimensions={2}, use_global_device_ids=true | all-gather | bytes 921600 | tf_op jit(solution)/shard_map/all_gather | solution.py:32
  134.8 23.6 %all-gather.9.cloned.1.call-done = bf16[1280,1280]{1,0:T(8,128)(2,1)} async-done(((bf16[320,1280]{1,0:T(8,128)(2,1)}), bf16[1280,1280]{1,0:T(8,128)(2,1)}) %all-gather.9.cloned.1.call-update) | async-done | bytes 3276816 | tf_op jit(solution)/shard_map/all_gather | solution.py:18
  158.4 6.2 %fusion.19 = bf16[3,1280,320]{1,2,0:T(8,128)(2,1)S(1)} fusion(bf16[1280,1280]{1,0:T(8,128)(2,1)} %all-gather.9.cloned.1.call-done, bf16[1,3,1280,320]{3,2,1,0:T(8,128)(2,1)} %all-gather.15.cloned.1.call-done, f32[3,320]{1,0:T(4,128)S(1)} %bitcast.60), kind=kOutput, calls=%fused_computation.38 | convolution fusion | flops 3148185600 | bytes 8195840 | tf_op jit(solution)/shard_map/rd,tdc->trc/dot_general | solution.py:22
  166.0 2.8 squeeze.21
  168.8 2.8 squeeze.22
  172.7 10.9 %fusion.49 = (f32[2,4,640]{2,1,0:T(4,128)S(1)}, f32[2,4,640,640]{2,3,1,0:T(8,128)}) fusion(pred[2,640,640]{1,2,0:T(8,128)(4,1)} %broadcast_compare_fusion, bf16[2,640,4,80]{1,0,3,2:T(2,128)(2,1)} %squeeze.22, bf16[2,640,4,80]{1,0,3,2:T(2,128)(2,1)} %squeeze.21), kind=kOutput, calls=%fused_computation.92 | convolution fusion | flops 537395840 | bytes 15585280 | tf_op jit(solution)/shard_map/sub | solution.py:51
  183.7 6.0 %fusion.28 = bf16[2,640,4,80]{1,3,2,0:T(8,128)(2,1)S(1)} fusion(f32[2,4,640,640]{2,3,1,0:T(8,128)} %get-tuple-element.13, f32[2,4,640]{2,1,0:T(4,128)S(1)} %get-tuple-element.12, bf16[2,640,4,80]{1,0,3,2:T(2,128)(2,1)S(1)} %copy-done.4), kind=kOutput, calls=%fused_computation.55 | convolution fusion | flops 531251200 | bytes 14766080 | tf_op jit(solution)/shard_map/bhqk,bkhe->bqhe/dot_general | solution.py:53
  190.8 3.6 convolution_convert_fusion.1
  195.4 44.3 %reduce-scatter.3.cloned.1.call-done = bf16[320,1280]{1,0:T(8,128)(2,1)} async-done(((bf16[1280,1280]{1,0:T(8,128)(2,1)}), bf16[320,1280]{1,0:T(8,128)(2,1)}) %reduce-scatter.3.cloned.1.call-update) | async-done | bytes 819216 | tf_op jit(solution)/shard_map/reduce_scatter | solution.py:34
  239.7 1.5 fusion.47
  241.2 1.6 multiply_reduce_fusion
  244.8 35.7 %all-gather.13.cloned.1.call-done = bf16[1,1280,1280]{2,1,0:T(8,128)(2,1)} async-done(((bf16[1,160,1280]{2,1,0:T(8,128)(2,1)}), bf16[1,1280,1280]{2,1,0:T(8,128)(2,1)}) %all-gather.13.cloned.1.call-update) | async-done | bytes 3276816 | tf_op jit(solution)/shard_map/all_gather | solution.py:25
  280.5 45.5 %all-gather.11.cloned.1.call-done = bf16[1280,1280]{1,0:T(8,128)(2,1)} async-done(((bf16[320,1280]{1,0:T(8,128)(2,1)}), bf16[1280,1280]{1,0:T(8,128)(2,1)}) %all-gather.11.cloned.1.call-update) | async-done | bytes 3276816 | tf_op jit(solution)/shard_map/all_gather | solution.py:18
  326.0 21.0 %fusion.4 = bf16[1280,1280]{1,0:T(8,128)(2,1)} fusion(bf16[1280,1280]{1,0:T(8,128)(2,1)} %all-gather.11.cloned.1.call-done, bf16[1,1280,1280]{2,1,0:T(8,128)(2,1)} %all-gather.13.cloned.1.call-done, f32[1280]{0:T(1024)S(1)} %reduce.9), kind=kOutput, calls=%fused_computation.14 | convolution fusion | flops 4302438400 | bytes 9835520 | tf_op jit(solution)/shard_map/rd,tdc->trc/dot_general | solution.py:22
  347.0 19.9 %all-gather.17.cloned.1.call-done = bf16[1,1280,1280]{1,2,0:T(8,128)(2,1)} async-done(((bf16[1,1280,160]{1,2,0:T(8,128)(2,1)}), bf16[1,1280,1280]{1,2,0:T(8,128)(2,1)}) %all-gather.17.cloned.1.call-update) | async-done | bytes 3276816 | tf_op jit(solution)/shard_map/all_gather | solution.py:32
  366.9 9.1 %convolution_convert_fusion = bf16[1280,1280]{1,0:T(8,128)(2,1)} fusion(bf16[1280,1280]{1,0:T(8,128)(2,1)} %fusion.4, bf16[1,1280,1280]{1,2,0:T(8,128)(2,1)} %all-gather.17.cloned.1.call-done), kind=kOutput, calls=%fused_computation.10 | convolution fusion | flops 4195942400 | bytes 9830400 | tf_op jit(solution)/shard_map/dot_general | solution.py:31
  376.7 43.3 %reduce-scatter.5.cloned.1.call-done = bf16[320,1280]{1,0:T(8,128)(2,1)} async-done(((bf16[1280,1280]{1,0:T(8,128)(2,1)}), bf16[320,1280]{1,0:T(8,128)(2,1)}) %reduce-scatter.5.cloned.1.call-update) | async-done | bytes 819216 | tf_op jit(solution)/shard_map/reduce_scatter | solution.py:34
  420.0 2.4 fusion.30
  (81 shorter events, 14.8 us)
Async XLA Ops:
  6.5 2.2 copy-start
  22.7 9.2 %copy-start.13 = (s32[256]{0:T(256)S(1)}, s32[256]{0:T(256)}, u32[]{:S(2)}) copy-start(s32[256]{0:T(256)} %param.18) | copy-start | bytes 3076
  22.7 9.3 %copy-start.8 = (s32[256]{0:T(256)S(1)}, s32[256]{0:T(256)}, u32[]{:S(2)}) copy-start(s32[256]{0:T(256)} %param.19) | copy-start | bytes 3076
  26.0 21.6 %all-to-all-start = ((bf16[512,4,320]{0,2,1:T(8,128)(2,1)}), bf16[512,4,320]{0,2,1:T(8,128)(2,1)S(1)}, u32[]{:S(2)}, u32[]{:S(2)}) async-start(bf16[512,4,320]{0,2,1:T(8,128)(2,1)} %add_convert_fusion.1), calls=%async_computation | async-start | bytes 2621440 | tf_op jit(solution)/shard_map/all_to_all | solution.py:131
  31.2 103.7 %all-gather.15.cloned.1.call-start = ((), (), s32[]{:S(2)}) async-start(), calls=%async_computation.10 | async-start | bytes 3317760 | tf_op jit(solution)/shard_map/all_gather | solution.py:25
  47.6 47.7 %copy-start.6 = (f32[1,2,1280]{2,1,0:T(2,128)S(1)}, f32[1,2,1280]{2,1,0:T(2,128)}, u32[]{:S(2)}) copy-start(f32[1,2,1280]{2,1,0:T(2,128)} %param.21) | copy-start | bytes 30724
  47.6 47.7 %copy-start.7 = (f32[1,2,1280]{2,1,0:T(2,128)S(1)}, f32[1,2,1280]{2,1,0:T(2,128)}, u32[]{:S(2)}) copy-start(f32[1,2,1280]{2,1,0:T(2,128)} %param.20) | copy-start | bytes 30724
  91.6 16.9 %all-to-all-start.2 = ((bf16[4,320,320]{2,1,0:T(8,128)(2,1)}), bf16[4,320,320]{2,1,0:T(8,128)(2,1)S(1)}, u32[]{:S(2)}, u32[]{:S(2)}) async-start(bf16[4,320,320]{2,1,0:T(8,128)(2,1)} %bitcast.7), calls=%async_computation.2 | async-start | bytes 1966080 | tf_op jit(solution)/shard_map/all_to_all | solution.py:139
  95.3 63.2 %all-gather.9.cloned.1.call-start = ((), (), s32[]{:S(2)}) async-start(), calls=%async_computation.5 | async-start | bytes 4096000 | tf_op jit(solution)/shard_map/all_gather | solution.py:18
  113.6 2.1 copy-start.12
  113.6 4.0 copy-start.5
  115.6 124.1 %reduce-scatter.3.cloned.1.call-start = ((), (), s32[]{:S(2)}) async-start(), calls=%async_computation.6 | async-start | bytes 4096000 | tf_op jit(solution)/shard_map/reduce_scatter | solution.py:34
  172.7 10.9 %copy-start.4 = (bf16[2,640,4,80]{1,0,3,2:T(2,128)(2,1)S(1)}, bf16[2,640,4,80]{1,0,3,2:T(2,128)(2,1)}, u32[]{:S(2)}) copy-start(bf16[2,640,4,80]{1,0,3,2:T(2,128)(2,1)} %squeeze.20) | copy-start | bytes 2457604
  189.6 1.2 copy-start.3
  194.5 0.9 copy-start.9
  194.5 86.0 %all-gather.13.cloned.1.call-start = ((), (), s32[]{:S(2)}) async-start(), calls=%async_computation.8 | async-start | bytes 3686400 | tf_op jit(solution)/shard_map/all_gather | solution.py:25
  195.1 131.0 %all-gather.11.cloned.1.call-start = ((), (), s32[]{:S(2)}) async-start(), calls=%async_computation.7 | async-start | bytes 4096000 | tf_op jit(solution)/shard_map/all_gather | solution.py:18
  239.7 3.1 copy-start.2
  241.2 3.6 copy-start.10
  244.1 122.7 %all-gather.17.cloned.1.call-start = ((), (), s32[]{:S(2)}) async-start(), calls=%async_computation.11 | async-start | bytes 3686400 | tf_op jit(solution)/shard_map/all_gather | solution.py:32
  244.7 175.3 %reduce-scatter.5.cloned.1.call-start = ((), (), s32[]{:S(2)}) async-start(), calls=%async_computation.9 | async-start | bytes 4096000 | tf_op jit(solution)/shard_map/reduce_scatter | solution.py:34
  375.9 0.7 copy-start.11
  375.9 46.5 %copy-start.1 = (bf16[256,1280]{1,0:T(8,128)(2,1)S(1)}, bf16[256,1280]{1,0:T(8,128)(2,1)}, u32[]{:S(2)}) copy-start(bf16[256,1280]{1,0:T(8,128)(2,1)} %param.16) | copy-start | bytes 1966084
Sparse Core Ops, SparseCore 0:
  33.6 40.4 all-gather.14
  115.7 42.7 all-gather.8
  194.6 44.9 reduce-scatter.2
  241.1 39.2 all-gather.12
  282.2 43.8 all-gather.10
  327.5 39.2 all-gather.16
  376.1 43.8 reduce-scatter.4
where the time goes:
time: 430 us; the launch traced here: 429 us
  waiting for transfers between devices  243 us (57%)
  matrix products  56.8 us (13%)
  blocking collectives  49.6 us (12%)
  local copies, waits for them, and re-layouts  40.6 us (9%)
  other arithmetic  16.6 us (4%)
  between operations  13.7 us (3%)
  starting transfers between devices  9.26 us (2%)
    reduce_scatter x2, waiting for transfers between devices, project_sum(): lax.psum_scatter(partials.astype(jnp.bfloat16), 'mp', scatter_dimension=0...  87.6 us
    all_gather x2, waiting for transfers between devices, gather_rows(): return lax.all_gather(normed, 'mp', axis=0, tiled=True)  69.2 us
    all_gather x2, waiting for transfers between devices, fold_rows(): lax.all_gather(weight, 'dp', axis=1, tiled=True)  35.7 us
    all_to_all x1, blocking collectives, per_device(): lax.all_to_all(buffer_rows, 'dp', split_axis=0, concat_axis=0, tiled=True)  32.4 us
    dot_general x2, matrix products, fold_rows(): jnp.einsum('rd,tdc->trc', gathered, lax.all_gather(weight, 'dp', axis=1,...  27.2 us
    all_gather x1, waiting for transfers between devices, project_sum(): lax.all_gather(weight, 'dp', axis=1, tiled=True)  19.9 us
    all_gather x1, blocking collectives, project_sum(): lax.all_gather(weight, 'dp', axis=1, tiled=True)  17.2 us
    all_to_all x1, waiting for transfers between devices, per_device(): lax.all_to_all(tokens.reshape(-1, column_count), 'mp', split_axis=1, conc...  15.4 us
  transfers between devices with their start and end apart: 9, of which 8 were waited for; matrix products, arithmetic and copies ran while one was open for 11% of the time, Pallas kernels for 0%

commit v1 on v0

--- a/solution.py
+++ b/solution.py
@@ -5,6 +5,11 @@
 from jax.sharding import PartitionSpec as P
 
 HEAD = 80
+
+
+def stack_and_merge(array, axis, dim):
+    blocks = lax.all_gather(array, axis)
+    return jnp.concatenate(blocks, axis=dim)
 
 
 def norm_rows(values, gain_row, shift_row):
@@ -22,7 +27,7 @@
     return jnp.einsum(
         "rd,tdc->trc",
         gathered,
-        lax.all_gather(weight, "dp", axis=1, tiled=True),
+        stack_and_merge(weight, "dp", 1),
         preferred_element_type=jnp.float32,
     )
 

time: 430 us -> 455 us (1.058); the launches traced: 429 us -> 446 us
  blocking collectives: 49.6 us -> 60.4 us
  waiting for transfers between devices: 243 us -> 249 us
    dot_general x2 -> x1, matrix products: 27.2 us -> 6.22 us  [fold_rows(): jnp.einsum('rd,tdc->trc', gathered, stack_and_merge(weight, 'dp', 1), pre...]
    dot_general x2, matrix products: 12.7 us -> 29.4 us  [project_sum(): jnp.dot(left, lax.all_gather(weight, 'dp', axis=1, tiled=True), preferred...]
    all_gather x1, waiting for transfers between devices: 19.9 us -> 36.3 us  [project_sum(): lax.all_gather(weight, 'dp', axis=1, tiled=True)]
    all_gather x2, waiting for transfers between devices: 69.2 us -> 54.6 us  [gather_rows(): return lax.all_gather(normed, 'mp', axis=0, tiled=True)]
    all_gather x1, blocking collectives: 17.2 us -> 28 us  [project_sum(): lax.all_gather(weight, 'dp', axis=1, tiled=True)]
  transfers between devices with their start and end apart: 9 -> 9, of which waited for: 8 -> 8; matrix products, arithmetic and copies ran while one was open for 11% -> 7% of each run, Pallas kernels for 0% -> 0%
where the time goes in v1:
time: 455 us; the launch traced here: 446 us
  waiting for transfers between devices  249 us (55%)
  blocking collectives  60.4 us (13%)
  matrix products  52.5 us (12%)
  local copies, waits for them, and re-layouts  44.5 us (10%)
  other arithmetic  16.6 us (4%)
  between operations  14.1 us (3%)
  starting transfers between devices  9.23 us (2%)
    reduce_scatter x2, waiting for transfers between devices, project_sum(): lax.psum_scatter(partials.astype(jnp.bfloat16), 'mp', scatter_dimension=0...  88.1 us
    all_gather x2, waiting for transfers between devices, gather_rows(): return lax.all_gather(normed, 'mp', axis=0, tiled=True)  54.6 us
    all_gather x2, waiting for transfers between devices, stack_and_merge(): blocks = lax.all_gather(array, axis)  39.7 us
    all_gather x1, waiting for transfers between devices, project_sum(): lax.all_gather(weight, 'dp', axis=1, tiled=True)  36.3 us
    all_to_all x1, blocking collectives, per_device(): lax.all_to_all(buffer_rows, 'dp', split_axis=0, concat_axis=0, tiled=True)  32.4 us
    dot_general x2, matrix products, project_sum(): jnp.dot(left, lax.all_gather(weight, 'dp', axis=1, tiled=True), preferred...  29.4 us
    all_gather x1, blocking collectives, project_sum(): lax.all_gather(weight, 'dp', axis=1, tiled=True)  28 us
    all_to_all x1, waiting for transfers between devices, per_device(): lax.all_to_all(tokens.reshape(-1, column_count), 'mp', split_axis=1, conc...  15.4 us
  transfers between devices with their start and end apart: 9, of which 8 were waited for; matrix products, arithmetic and copies ran while one was open for 7% of the time, Pallas kernels for 0%

profile of v1, /device:TPU:0, one launch (start us, length us, event | category | flops | bytes accessed | tf_op | source)
XLA Modules:
  0.0 446.4 jit_solution(8761019695922364255)
XLA Ops:
  8.8 2.1 gather_fusion
  10.9 1.5 copy.57
  12.5 8.7 %gather_fusion.1 = bf16[512,1280]{1,0:T(8,128)(2,1)S(1)} fusion(bf16[8,256,1280]{2,1,0:T(8,128)(2,1)} %param.15, s32[512]{0:T(512)S(1)} %reshape.200), kind=kCustom, calls=%fused_computation.1 | custom fusion | bytes 2625536 | tf_op jit(solution)/shard_map/jit(take_along_axis)/gather | solution.py:119
  21.1 1.5 copy.56
  22.7 3.3 add_convert_fusion.1
  26.0 5.2 %all-to-all-start = ((bf16[512,4,320]{0,2,1:T(8,128)(2,1)}), bf16[512,4,320]{0,2,1:T(8,128)(2,1)S(1)}, u32[]{:S(2)}, u32[]{:S(2)}) async-start(bf16[512,4,320]{0,2,1:T(8,128)(2,1)} %add_convert_fusion.1), calls=%async_computation | async-start | bytes 2621440 | tf_op jit(solution)/shard_map/all_to_all | solution.py:136
  32.2 15.4 %all-to-all-done = bf16[512,4,320]{0,2,1:T(8,128)(2,1)S(1)} async-done(((bf16[512,4,320]{0,2,1:T(8,128)(2,1)}), bf16[512,4,320]{0,2,1:T(8,128)(2,1)S(1)}, u32[]{:S(2)}, u32[]{:S(2)}) %all-to-all-start) | async-done | bytes 1310752 | tf_op jit(solution)/shard_map/all_to_all | solution.py:136
  47.6 1.6 copy.70
  49.2 10.0 %scatter_custom_fusion = bf16[1280,320]{1,0:T(8,128)(2,1)S(1)} fusion(s32[2048]{0:T(1024)S(1)} %bitcast.58, bf16[2048,320]{1,0:T(8,128)(2,1)} %bitcast.56, bf16[]{:T(256)} %constant.58.clone.1), kind=kCustom, calls=%fused_computation.62 | custom fusion | bytes 819712 | tf_op jit(solution)/shard_map/scatter | solution.py:142
  59.2 32.4 %all_to_all.38 = bf16[8,160,320]{2,1,0:T(8,128)(2,1)} all-to-all(bf16[8,160,320]{2,1,0:T(8,128)(2,1)S(1)} %bitcast.52), channel_id=1, replica_groups=mesh['dp'=8,'mp'=4] {'dp'}, dimensions={0} | all-to-all | bytes 1638400 | tf_op jit(solution)/shard_map/all_to_all | solution.py:145
  91.6 3.7 all-to-all-start.2
  95.4 13.2 %all-to-all-done.2 = bf16[4,320,320]{2,1,0:T(8,128)(2,1)S(1)} async-done(((bf16[4,320,320]{2,1,0:T(8,128)(2,1)}), bf16[4,320,320]{2,1,0:T(8,128)(2,1)S(1)}, u32[]{:S(2)}, u32[]{:S(2)}) %all-to-all-start.2) | async-done | bytes 819232 | tf_op jit(solution)/shard_map/all_to_all | solution.py:144
  108.7 2.5 copy.60
  111.2 2.4 reshape.191
  117.6 28.0 %all-gather = bf16[1,320,1280]{1,2,0:T(8,128)(2,1)} all-gather(bf16[1,320,160]{1,2,0:T(8,128)(2,1)S(1)} %copy-done.5), channel_id=2, replica_groups=mesh['dp'=8,'mp'=4] {'dp'}, dimensions={2}, use_global_device_ids=true | all-gather | bytes 921600 | tf_op jit(solution)/shard_map/all_gather | solution.py:37
  145.6 3.9 copy.61
  149.5 9.0 %all-gather.9.cloned.1.call-done = bf16[1280,1280]{1,0:T(8,128)(2,1)} async-done(((bf16[320,1280]{1,0:T(8,128)(2,1)}), bf16[1280,1280]{1,0:T(8,128)(2,1)}) %all-gather.9.cloned.1.call-update) | async-done | bytes 3276816 | tf_op jit(solution)/shard_map/all_gather | solution.py:23
  158.5 6.2 %fusion.18 = bf16[3,1280,320]{1,2,0:T(8,128)(2,1)S(1)} fusion(bf16[3,1280,320]{2,1,0:T(8,128)(2,1)} %bitcast.55, bf16[1280,1280]{1,0:T(8,128)(2,1)} %all-gather.9.cloned.1.call-done, f32[3,320]{1,0:T(4,128)S(1)} %bitcast.59), kind=kOutput, calls=%fused_computation.37 | convolution fusion | flops 3148185600 | bytes 8195840 | tf_op jit(solution)/shard_map/rd,tdc->trc/dot_general | solution.py:27
  166.1 2.8 squeeze.17
  168.9 2.8 squeeze.18
  172.8 10.9 %fusion.77 = (f32[2,4,640]{2,1,0:T(4,128)S(1)}, f32[2,4,640,640]{2,3,1,0:T(8,128)}) fusion(pred[2,640,640]{1,2,0:T(8,128)(4,1)} %broadcast_compare_fusion, bf16[2,640,4,80]{1,0,3,2:T(2,128)(2,1)} %squeeze.18, bf16[2,640,4,80]{1,0,3,2:T(2,128)(2,1)} %squeeze.17), kind=kOutput, calls=%fused_computation.120 | convolution fusion | flops 537395840 | bytes 15585280 | tf_op jit(solution)/shard_map/sub | solution.py:56
  183.7 6.0 %fusion.26 = bf16[2,640,4,80]{1,3,2,0:T(8,128)(2,1)S(1)} fusion(f32[2,4,640,640]{2,3,1,0:T(8,128)} %get-tuple-element.13, f32[2,4,640]{2,1,0:T(4,128)S(1)} %get-tuple-element.12, bf16[2,640,4,80]{1,0,3,2:T(2,128)(2,1)S(1)} %copy-done.4), kind=kOutput, calls=%fused_computation.53 | convolution fusion | flops 531251200 | bytes 14766080 | tf_op jit(solution)/shard_map/bhqk,bkhe->bqhe/dot_general | solution.py:58
  190.9 3.7 convolution_convert_fusion.1
  196.0 43.7 %reduce-scatter.3.cloned.1.call-done = bf16[320,1280]{1,0:T(8,128)(2,1)} async-done(((bf16[1280,1280]{1,0:T(8,128)(2,1)}), bf16[320,1280]{1,0:T(8,128)(2,1)}) %reduce-scatter.3.cloned.1.call-update) | async-done | bytes 819216 | tf_op jit(solution)/shard_map/reduce_scatter | solution.py:39
  239.7 1.5 fusion.75
  241.3 1.6 multiply_reduce_fusion
  244.3 36.3 %all-gather.17.cloned.1.call-done = bf16[1,1280,1280]{1,2,0:T(8,128)(2,1)} async-done(((bf16[1,1280,160]{1,2,0:T(8,128)(2,1)}), bf16[1,1280,1280]{1,2,0:T(8,128)(2,1)}) %all-gather.17.cloned.1.call-update) | async-done | bytes 3276816 | tf_op jit(solution)/shard_map/all_gather | solution.py:37
  280.6 39.7 %all-gather.15.cloned.1.call-done = bf16[8,160,1280]{2,1,0:T(8,128)(2,1)} async-done(((bf16[1,160,1280]{2,1,0:T(8,128)(2,1)}), bf16[8,160,1280]{2,1,0:T(8,128)(2,1)}) %all-gather.15.cloned.1.call-update) | async-done | bytes 3276816 | tf_op jit(solution)/shard_map/all_gather | solution.py:11
  320.3 45.6 %all-gather.13.cloned.1.call-done = bf16[1280,1280]{1,0:T(8,128)(2,1)} async-done(((bf16[320,1280]{1,0:T(8,128)(2,1)}), bf16[1280,1280]{1,0:T(8,128)(2,1)}) %all-gather.13.cloned.1.call-update) | async-done | bytes 3276816 | tf_op jit(solution)/shard_map/all_gather | solution.py:23
  365.8 25.7 %convolution_convert_fusion = bf16[1280,1280]{1,0:T(8,128)(2,1)} fusion(bf16[1,1280,1280]{1,2,0:T(8,128)(2,1)} %all-gather.17.cloned.1.call-done, bf16[1280,1280]{1,0:T(8,128)(2,1)} %all-gather.13.cloned.1.call-done, bf16[1280,1280]{1,0:T(8,128)(2,1)} %bitcast.60, f32[1280]{0:T(1024)S(1)} %reduce.9), kind=kOutput, calls=%fused_computation.10 | convolution fusion | flops 8498380800 | bytes 13112320 | tf_op jit(solution)/shard_map/dot_general | solution.py:36
  392.3 44.4 %reduce-scatter.5.cloned.1.call-done = bf16[320,1280]{1,0:T(8,128)(2,1)} async-done(((bf16[1280,1280]{1,0:T(8,128)(2,1)}), bf16[320,1280]{1,0:T(8,128)(2,1)}) %reduce-scatter.5.cloned.1.call-update) | async-done | bytes 819216 | tf_op jit(solution)/shard_map/reduce_scatter | solution.py:39
  436.7 2.4 fusion.28
  (81 shorter events, 14.8 us)
Async XLA Ops:
  6.5 2.2 copy-start
  22.7 9.2 %copy-start.13 = (s32[256]{0:T(256)S(1)}, s32[256]{0:T(256)}, u32[]{:S(2)}) copy-start(s32[256]{0:T(256)} %param.18) | copy-start | bytes 3076
  22.7 9.3 %copy-start.8 = (s32[256]{0:T(256)S(1)}, s32[256]{0:T(256)}, u32[]{:S(2)}) copy-start(s32[256]{0:T(256)} %param.19) | copy-start | bytes 3076
  26.0 21.6 %all-to-all-start = ((bf16[512,4,320]{0,2,1:T(8,128)(2,1)}), bf16[512,4,320]{0,2,1:T(8,128)(2,1)S(1)}, u32[]{:S(2)}, u32[]{:S(2)}) async-start(bf16[512,4,320]{0,2,1:T(8,128)(2,1)} %add_convert_fusion.1), calls=%async_computation | async-start | bytes 2621440 | tf_op jit(solution)/shard_map/all_to_all | solution.py:136
  31.2 114.5 %all-gather.11.cloned.1.call-start = ((), (), s32[]{:S(2)}) async-start(), calls=%async_computation.6 | async-start | bytes 3317760 | tf_op jit(solution)/shard_map/all_gather | solution.py:11
  47.6 47.7 %copy-start.6 = (f32[1,2,1280]{2,1,0:T(2,128)S(1)}, f32[1,2,1280]{2,1,0:T(2,128)}, u32[]{:S(2)}) copy-start(f32[1,2,1280]{2,1,0:T(2,128)} %param.21) | copy-start | bytes 30724
  47.6 47.7 %copy-start.7 = (f32[1,2,1280]{2,1,0:T(2,128)S(1)}, f32[1,2,1280]{2,1,0:T(2,128)}, u32[]{:S(2)}) copy-start(f32[1,2,1280]{2,1,0:T(2,128)} %param.20) | copy-start | bytes 30724
  91.6 16.9 %all-to-all-start.2 = ((bf16[4,320,320]{2,1,0:T(8,128)(2,1)}), bf16[4,320,320]{2,1,0:T(8,128)(2,1)S(1)}, u32[]{:S(2)}, u32[]{:S(2)}) async-start(bf16[4,320,320]{2,1,0:T(8,128)(2,1)} %bitcast.7), calls=%async_computation.2 | async-start | bytes 1966080 | tf_op jit(solution)/shard_map/all_to_all | solution.py:144
  95.3 63.2 %all-gather.9.cloned.1.call-start = ((), (), s32[]{:S(2)}) async-start(), calls=%async_computation.5 | async-start | bytes 4096000 | tf_op jit(solution)/shard_map/all_gather | solution.py:23
  113.6 2.1 copy-start.12
  113.6 4.0 copy-start.5
  115.6 124.1 %reduce-scatter.3.cloned.1.call-start = ((), (), s32[]{:S(2)}) async-start(), calls=%async_computation.7 | async-start | bytes 4096000 | tf_op jit(solution)/shard_map/reduce_scatter | solution.py:39
  172.8 10.9 %copy-start.4 = (bf16[2,640,4,80]{1,0,3,2:T(2,128)(2,1)S(1)}, bf16[2,640,4,80]{1,0,3,2:T(2,128)(2,1)}, u32[]{:S(2)}) copy-start(bf16[2,640,4,80]{1,0,3,2:T(2,128)(2,1)} %squeeze.16) | copy-start | bytes 2457604
  189.7 1.2 copy-start.3
  194.5 1.4 copy-start.9
  194.6 86.0 %all-gather.17.cloned.1.call-start = ((), (), s32[]{:S(2)}) async-start(), calls=%async_computation.11 | async-start | bytes 3686400 | tf_op jit(solution)/shard_map/all_gather | solution.py:37
  195.1 125.1 %all-gather.15.cloned.1.call-start = ((), (), s32[]{:S(2)}) async-start(), calls=%async_computation.10 | async-start | bytes 3686400 | tf_op jit(solution)/shard_map/all_gather | solution.py:11
  195.7 170.1 %all-gather.13.cloned.1.call-start = ((), (), s32[]{:S(2)}) async-start(), calls=%async_computation.8 | async-start | bytes 4096000 | tf_op jit(solution)/shard_map/all_gather | solution.py:23
  239.7 3.1 copy-start.2
  241.3 3.0 copy-start.10
  244.2 192.5 %reduce-scatter.5.cloned.1.call-start = ((), (), s32[]{:S(2)}) async-start(), calls=%async_computation.9 | async-start | bytes 4096000 | tf_op jit(solution)/shard_map/reduce_scatter | solution.py:39
  391.5 0.7 copy-start.11
  391.5 47.6 %copy-start.1 = (bf16[256,1280]{1,0:T(8,128)(2,1)S(1)}, bf16[256,1280]{1,0:T(8,128)(2,1)}, u32[]{:S(2)}) copy-start(bf16[256,1280]{1,0:T(8,128)(2,1)} %param.16) | copy-start | bytes 1966084
Sparse Core Ops, SparseCore 0:
  33.6 40.5 all-gather.10
  115.7 42.7 all-gather.8
  194.7 44.9 reduce-scatter.2
  241.2 39.2 all-gather.16
  282.0 38.1 all-gather.14
  322.0 43.8 all-gather.12
  391.7 44.9 reduce-scatter.4
